TPU v7x, 256 devices: a 8x8x2 block of a 8x8x16 slice. The times are simulated.
256 devices in a mesh: grp: 2 (over z), win: 128 (over y, x, core).
Axes of the slice: x: 8, y: 8, z: 2, core: 2. Of those that a mesh axis runs over, the one named last changes fastest.
The devices are a block of a 8x8x16 slice.
Arguments:
- tokens: bfloat16 [4, 8, 64, 384, 384], P('grp', None, None, 'win'), parts along dimension 0, may hold values from -6 to 6
- w_upper: bfloat16 [384, 640], replicated, may hold values from -0.3125 to 0.3125
- w_surface: bfloat16 [384, 256], replicated, may hold values from -0.3125 to 0.3125
- bias: float32 [69], replicated, may hold values from -1 to 1
Outputs:
- fields: bfloat16 [4, 17664, 1536], P('grp', 'win'), parts along dimension 0
There are 2 independent parts, one for each index of `grp`. A program takes and returns all parts, laid end to end along the dimension named above; an argument that names none is the same for every part. Nothing has to cross between parts.
All inputs are finite; a program needn't handle non-finite values.
Results may differ from a plain program's by a relative error of at most 0.0048.
Values may be sent and summed in bfloat16 or wider, within the bound.
A program may use at most 128 MiB of HBM per device.

v0:
```python
import jax
import jax.numpy as jnp
from jax import lax
from jax.sharding import Mesh
from jax.sharding import PartitionSpec as P

VARS_UP = 5
LEVELS = 13
VARS_SF = 4
PATCH = 4
WIN = ("win_0", "win_1", "win_2")


def shifted(x, axis, by):
    size = lax.axis_size(axis)
    return lax.ppermute(x, axis, [(i, (i + by) % size) for i in range(size)])


def in_blocks(x, dim, size):
    before, after = (x.shape[:dim], x.shape[dim + 1 :])
    return jnp.moveaxis(x.reshape(*before, size, -1, *after), dim, 0)


def in_order(parts, dim):
    shape = list(parts.shape[1:])
    shape[dim] *= parts.shape[0]
    return jnp.moveaxis(parts, 0, dim).reshape(shape)


def moved_by_axis(parts, axes, turns):
    inside = parts.shape[1:]
    result = parts.reshape(*(lax.axis_size(a) for a in axes), *inside)
    for k in turns:
        result = lax.all_to_all(result, axes[k], k, k, tiled=True)
    return result.reshape(-1, *inside)


def exchange_by_chip(x, groups, turns, split_dim, concat_dim):
    size = lax.axis_size(groups[0]) * lax.axis_size(groups[1])
    parts = in_blocks(x, split_dim, size)
    return in_order(moved_by_axis(parts, groups, turns), concat_dim)


def intersection_add(values, axis):
    first = lax.index_in_dim(values, 0, axis + 1, keepdims=False)
    second = lax.index_in_dim(values, 1, axis + 1, keepdims=False)
    pad_first = [(0, 0)] * first.ndim
    pad_second = [(0, 0)] * first.ndim
    pad_first[axis] = (0, 1)
    pad_second[axis] = (1, 0)
    return jnp.pad(first, pad_first) + jnp.pad(second, pad_second)


def latitude_add(values):
    first = values[..., 0, :, :]
    second = values[..., 1, :, :]
    pad_first = [(0, 0)] * (first.ndim - 1) + [(0, 1)]
    pad_second = [(0, 0)] * (first.ndim - 1) + [(1, 0)]
    summed = jnp.pad(first, pad_first) + jnp.pad(second, pad_second)
    return jnp.swapaxes(summed, -1, -2)


def project(tokens, w_upper, w_surface):
    members, tok_levels, lat_rows, lon_cols, width = tokens.shape
    upper_levels = tok_levels - 1
    rim_width = PATCH // 2
    frame_width = (lon_cols + 1) * PATCH
    upper_tok = jnp.transpose(tokens[:, :upper_levels], (0, 1, 3, 4, 2))
    kernel_up = w_upper.reshape(width, VARS_UP, 2, 2, PATCH, 2, PATCH)
    upper = jnp.einsum(
        "dvlpqrs,mzjdi->vlpqrsmzji", kernel_up, upper_tok, preferred_element_type=jnp.float32
    )
    upper = jnp.transpose(upper, (6, 8, 4, 5, 0, 7, 1, 2, 3, 9))
    upper = intersection_add(upper, 1)
    upper = latitude_add(upper)
    upper = upper.reshape(members, frame_width, VARS_UP, 2 * upper_levels, (lat_rows + 1) * PATCH)
    upper = upper[:, :, :, :LEVELS, rim_width : rim_width + lat_rows * PATCH]
    upper = upper.reshape(members, frame_width, VARS_UP * LEVELS, lat_rows * PATCH)
    surface_tok = jnp.transpose(tokens[:, upper_levels], (0, 2, 3, 1))
    kernel_sf = w_surface.reshape(width, VARS_SF, 2, PATCH, 2, PATCH)
    surface = jnp.einsum(
        "dvpqrs,mjdi->vpqrsmji", kernel_sf, surface_tok, preferred_element_type=jnp.float32
    )
    surface = jnp.transpose(surface, (5, 6, 3, 4, 0, 1, 2, 7))
    surface = intersection_add(surface, 1)
    surface = latitude_add(surface)
    surface = surface.reshape(members, frame_width, VARS_SF, (lat_rows + 1) * PATCH)
    surface = surface[:, :, :, rim_width : rim_width + lat_rows * PATCH]
    joined = jnp.concatenate([upper, surface], axis=2).astype(jnp.bfloat16)
    return joined.reshape(members, frame_width, -1)


def deliver(frames, bias, lat_rows):
    rim_width = PATCH // 2
    members, frame_width, all_rows = frames.shape
    columns = frame_width - 2 * rim_width
    from_left = shifted(frames[:, frame_width - rim_width :, :], WIN, 1)
    from_right = shifted(frames[:, :rim_width, :], WIN, -1)
    inner = frames[:, rim_width : frame_width - rim_width, :].astype(jnp.float32)
    summed = inner + jnp.pad(
        from_left.astype(jnp.float32), ((0, 0), (0, columns - rim_width), (0, 0))
    )
    summed = summed + jnp.pad(
        from_right.astype(jnp.float32), ((0, 0), (columns - rim_width, 0), (0, 0))
    )
    bias_rows = jnp.repeat(bias, lat_rows * PATCH)
    image = (summed + bias_rows[None, None, :]).astype(jnp.bfloat16)
    received = exchange_by_chip(image, (("win_0", "win_1"), "win_2"), (0, 1), 2, 1)
    return jnp.transpose(received, (0, 2, 1))


def body(tokens, w_upper, w_surface, bias):
    lat_rows = tokens.shape[2]
    frames = project(tokens, w_upper, w_surface)
    return deliver(frames, bias, lat_rows)


def solution(mesh):
    torus = Mesh(
        mesh.devices.reshape(mesh.shape["grp"], 8, 8, 2), ("grp", "win_0", "win_1", "win_2")
    )
    placed = (P("grp", None, None, WIN, None), P(), P(), P())
    return jax.shard_map(
        body, mesh=torus, in_specs=placed, out_specs=P("grp", WIN, None), check_vma=False
    )
```

profile of v0, /device:TPU:513, one launch (start us, length us, event | category | flops | bytes accessed | tf_op | source)
XLA Modules:
  0.0 206.1 jit_solution(5679282979167281423)
XLA Ops:
  0.0 1.3 copy.55
  1.3 0.1 reshape.34
  1.4 7.5 %convolution_bitcast_fusion = f32[2,3,2,4,5,7,2,2,4,64]{9,4,1,5,0,3,2,8,7,6:T(8,128)S(1)} fusion(bf16[2,8,64,3,384]{4,2,3,1,0:T(8,128)(2,1)} %param.4, bf16[384,5,2,2,4,2,4,1,1,1]{0,6,5,4,3,2,1,9,8,7:T(4,128)(2,1)S(1)} %bitcast.83), kind=kOutput, calls=%fused_computation.4 | convolution fusion | flops 1321205760 | bytes 9437184 | tf_op jit(solution)/shard_map/dvlpqrs,mzjdi->vlpqrsmzji/dot_general | solution.py:70
  8.9 8.7 %slice_bitcast_fusion.1 = (f32[2,3,4,5,7,2,2,4,64]{8,3,1,4,0,2,7,6,5:T(8,128)}, f32[2,3,4,5,7,2,2,4,64]{8,3,1,4,0,2,7,6,5:T(8,128)}) fusion(f32[2,3,2,4,5,7,2,2,4,64]{9,4,1,5,0,3,2,8,7,6:T(8,128)S(1)} %convolution_bitcast_fusion), kind=kLoop, calls=%fused_computation.3 | loop fusion | bytes 13762560 | tf_op jit(solution)/shard_map/squeeze | solution.py:45
  17.6 12.0 %fusion.1 = (f32[2,4,4,5,7,2,4,64]{7,3,1,4,0,2,6,5:T(8,128)S(1)}, f32[2,4,4,5,7,2,4,64]{7,3,1,4,0,2,6,5:T(8,128)}) fusion(f32[2,3,4,5,7,2,2,4,64]{8,3,1,4,0,2,7,6,5:T(8,128)} %get-tuple-element.7, f32[2,3,4,5,7,2,2,4,64]{8,3,1,4,0,2,7,6,5:T(8,128)} %get-tuple-element.8), kind=kLoop, calls=%fused_computation.6 | loop fusion | flops 1146880 | bytes 11468800 | tf_op jit(solution)/shard_map/squeeze | solution.py:55
  29.6 6.9 %fusion.3 = bf16[2,4,4,5,7,2,65,4]{6,3,1,4,0,2,7,5:T(8,128)(2,1)} fusion(f32[2,4,4,5,7,2,4,64]{7,3,1,4,0,2,6,5:T(8,128)} %get-tuple-element.6, f32[2,4,4,5,7,2,4,64]{7,3,1,4,0,2,6,5:T(8,128)S(1)} %get-tuple-element.5), kind=kLoop, calls=%fused_computation.10 | loop fusion | flops 1164800 | bytes 5752320 | tf_op jit(solution)/shard_map/transpose | solution.py:60
  36.4 31.1 %copy.59 = bf16[2,4,4,5,7,2,65,4]{7,6,2,1,5,4,3,0:T(8,128)(2,1)} copy(bf16[2,4,4,5,7,2,65,4]{6,3,1,4,0,2,7,5:T(8,128)(2,1)} %fusion.3) | data formatting | bytes 2329600 | tf_op jit(solution)/shard_map/transpose | solution.py:60
  67.5 0.0 copy-start
  67.5 39.4 %reshape.35 = bf16[2,16,5,14,260]{4,1,3,2,0:T(8,128)(2,1)S(1)} reshape(bf16[2,4,4,5,7,2,65,4]{7,6,2,1,5,4,3,0:T(8,128)(2,1)} %copy.59) | data formatting | bytes 2329600 | tf_op jit(solution)/shard_map/reshape | solution.py:76
  106.9 0.4 slice.66
  107.3 0.0 copy-done
  107.3 0.2 copy.60
  107.5 0.1 reshape.45
  107.6 1.4 convolution_bitcast_fusion.1
  109.0 0.1 slice_bitcast_fusion.3
  109.1 0.2 fusion.10
  109.3 0.2 fusion.13
  109.5 1.2 copy.64
  110.8 1.3 reshape.38
  112.0 0.1 slice.71
  112.1 0.0 copy-start.1
  112.1 0.1 maximum_bitcast_fusion
  112.2 0.1 copy.82
  112.3 0.2 fusion.14
  112.6 2.8 %collective-permute-start = (bf16[2,2,17664]{2,1,0:T(2,128)(2,1)S(1)}, bf16[2,2,17664]{2,1,0:T(2,128)(2,1)S(1)}, u32[]{:S(2)}, u32[]{:S(2)}) collective-permute-start(bf16[2,2,17664]{2,1,0:T(2,128)(2,1)S(1)} %get-tuple-element.9), channel_id=1, source_target_pairs={{0,1},{1,2},{2,3},{3,4},{4,5},{5,6},{6,7},{7,8},{8,9},{9,10},{10,1... | collective-permute-start | bytes 423944 | tf_op jit(solution)/shard_map/ppermute | solution.py:16
  115.3 17.9 %collective-permute-start.1 = (bf16[2,2,17664]{2,1,0:T(2,128)(2,1)S(1)}, bf16[2,2,17664]{2,1,0:T(2,128)(2,1)S(1)}, u32[]{:S(2)}, u32[]{:S(2)}) collective-permute-start(bf16[2,2,17664]{2,1,0:T(2,128)(2,1)S(1)} %get-tuple-element.10), channel_id=1, source_target_pairs={{0,127},{1,0},{2,1},{3,2},{4,3},{5,4},{6,5},{7,6},{8,7},{9,8},{10,... | collective-permute-start | bytes 423944 | tf_op jit(solution)/shard_map/ppermute | solution.py:16
  133.2 0.0 copy-done.1
  133.2 0.1 broadcast_in_dim.3
  133.3 0.6 collective-permute-done
  134.0 0.3 collective-permute-done.1
  134.2 0.6 add_convert_fusion.1
  134.9 0.7 copy.66
  135.5 4.7 %reshape.39 = bf16[2,12,128,138]{3,2,0,1:T(8,128)(2,1)S(1)} reshape(bf16[2,12,17664]{2,0,1:T(2,128)(2,1)S(1)} %copy.66) | data formatting | bytes 1695744 | tf_op jit(solution)/shard_map/reshape | solution.py:21
  140.3 1.6 copy.67
  141.9 53.3 %all_to_all.10 = bf16[64,2,2,12,138]{4,2,3,1,0:T(2,128)(2,1)S(1)} all-to-all(bf16[64,2,2,12,138]{4,2,3,1,0:T(2,128)(2,1)S(1)} %bitcast.78), channel_id=1, replica_groups=mesh['grp'=2,'win_0'=8,'win_1'=8,'win_2'=2] {'win_0','win_1'}, dimensions={0} | all-to-all | bytes 1695744 | tf_op jit(solution)/shard_map/all_to_all | solution.py:34
  195.1 1.1 copy.68
  196.2 4.7 %all_to_all.11 = bf16[64,2,2,12,138]{4,2,3,0,1:T(2,128)(2,1)S(1)} all-to-all(bf16[64,2,2,12,138]{4,2,3,0,1:T(2,128)(2,1)S(1)} %copy.68), channel_id=1, replica_groups=mesh['grp'=2,'win_0'=8,'win_1'=8,'win_2'=2] {'win_2'}, dimensions={1} | all-to-all | bytes 1695744 | tf_op jit(solution)/shard_map/all_to_all | solution.py:34
  200.9 1.1 copy.69
  202.0 4.1 %copy.70 = bf16[2,138,1536]{2,0,1:T(2,128)(2,1)} copy(bf16[2,138,1536]{1,0,2:T(2,128)(2,1)S(1)} %bitcast.79) | data formatting | bytes 1695744 | tf_op jit(solution)/shard_map/transpose | solution.py:109
  (1 shorter events, 0.0 us)
Async XLA Ops:
  67.5 39.8 %copy-start = (bf16[384,256]{1,0:T(8,128)(2,1)S(1)}, bf16[384,256]{1,0:T(8,128)(2,1)}, u32[]{:S(2)}) copy-start(bf16[384,256]{1,0:T(8,128)(2,1)} %param.6) | copy-start | bytes 589828
  112.1 21.1 %copy-start.1 = (f32[69]{0:T(128)S(1)}, f32[69]{0:T(128)}, u32[]{:S(2)}) copy-start(f32[69]{0:T(128)} %param.7) | copy-start | bytes 832
  112.6 21.4 %collective-permute-start = (bf16[2,2,17664]{2,1,0:T(2,128)(2,1)S(1)}, bf16[2,2,17664]{2,1,0:T(2,128)(2,1)S(1)}, u32[]{:S(2)}, u32[]{:S(2)}) collective-permute-start(bf16[2,2,17664]{2,1,0:T(2,128)(2,1)S(1)} %get-tuple-element.9), channel_id=1, source_target_pairs={{0,1},{1,2},{2,3},{3,4},{4,5},{5,6},{6,7},{7,8},{8,9},{9,10},{10,1... | collective-permute-start | bytes 423944 | tf_op jit(solution)/shard_map/ppermute | solution.py:16
  115.3 18.9 %collective-permute-start.1 = (bf16[2,2,17664]{2,1,0:T(2,128)(2,1)S(1)}, bf16[2,2,17664]{2,1,0:T(2,128)(2,1)S(1)}, u32[]{:S(2)}, u32[]{:S(2)}) collective-permute-start(bf16[2,2,17664]{2,1,0:T(2,128)(2,1)S(1)} %get-tuple-element.10), channel_id=1, source_target_pairs={{0,127},{1,0},{2,1},{3,2},{4,3},{5,4},{6,5},{7,6},{8,7},{9,8},{10,... | collective-permute-start | bytes 423944 | tf_op jit(solution)/shard_map/ppermute | solution.py:16
where the time goes:
time: 208 us; the launch traced here: 206 us
  local copies, waits for them, and re-layouts  97.5 us (47%)
  blocking collectives  57.9 us (28%)
  starting transfers between devices  20.7 us (10%)
  other arithmetic  20 us (10%)
  matrix products  8.92 us (4%)
    all_to_all x2, blocking collectives, moved_by_axis(): result = lax.all_to_all(result, axes[k], k, k, tiled=True)  57.9 us
    reshape x1, local copies, waits for them, and re-layouts, project(): upper.reshape(members, frame_width, VARS_UP, 2 * upper_levels, (lat_rows...  39.4 us
    transpose x2, local copies, waits for them, and re-layouts, latitude_add(): return jnp.swapaxes(summed, -1, -2)  32.3 us
    ppermute x2, starting transfers between devices, shifted(): return lax.ppermute(x, axis, [(i, (i + by) % size) for i in range(size)])  20.7 us
    squeeze x2, other arithmetic, latitude_add(): first = values[..., 0, :, :]  12.2 us
    squeeze x2, local copies, waits for them, and re-layouts, intersection_add(): first = lax.index_in_dim(values, 0, axis + 1, keepdims=False)  8.78 us
    dot_general x1, matrix products, project(): jnp.einsum('dvlpqrs,mzjdi->vlpqrsmzji', kernel_up, upper_tok, preferred_e...  7.48 us
    transpose x2, other arithmetic, latitude_add(): return jnp.swapaxes(summed, -1, -2)  7.06 us
  transfers between devices with their start and end apart: 2, of which 2 were waited for; matrix products, arithmetic and copies ran while one was open for 0% of the time, Pallas kernels for 0%

commit v1 on v0

v1 whole, which is shorter than its diff:
```python
import functools

import jax
import jax.numpy as jnp
from jax import lax
from jax.experimental import pallas as pl
from jax.experimental.pallas import tpu as pltpu
from jax.sharding import PartitionSpec as P

MESH = pl.DeviceIdType.MESH
BF = jnp.bfloat16
F32 = jnp.float32
VARS_UP = 5
LEVELS = 13
VARS_SF = 4
CHANNELS = VARS_UP * LEVELS + VARS_SF
LAT = 256
ROWS = CHANNELS * LAT // 128
TILES = ROWS + 2
NT = (((1,), (1,)), ((), ()))
SIDE = 8


def step_of(dy, dx):
    return ((dy - dx + SIDE) % SIDE) * SIDE + dx


def offset_of(s):
    dx = s % SIDE
    return (s // SIDE + dx) % SIDE, dx


def kernel_weights(w, kinds):
    width = w.shape[0]
    wt = jnp.transpose(w.reshape(width, kinds, 8, 8), (2, 1, 3, 0))

    def rows(lo, hi, before, after):
        return jnp.pad(wt[:, :, lo:hi], ((0, 0), (0, 0), (before, after), (0, 0)))

    def join(*parts):
        return jnp.concatenate(parts, -1).reshape(-1, width * len(parts))

    last = join(rows(6, 8, 0, 6), rows(2, 8, 0, 2), rows(0, 6, 2, 0))
    first = join(rows(2, 6, 0, 0), rows(0, 2, 2, 0))
    rims = join(rows(0, 2, 2, 0), rows(6, 8, 0, 2))
    return last, first, rims


def latitude(product_ref, kinds_rows, lane0):
    lane = lax.broadcasted_iota(jnp.int32, (1, 128), 1) % 64
    parts = []
    for b in range(4):
        main = product_ref[(b + 2) * kinds_rows : (b + 3) * kinds_rows, lane0 : lane0 + 128]
        a = (b + 6) % 8
        other = product_ref[a * kinds_rows : (a + 1) * kinds_rows, lane0 : lane0 + 128]
        if b < 2:
            moved = jnp.where(lane != 0, pltpu.roll(other, 1, 1), 0.0)
        else:
            moved = jnp.where(lane != 63, pltpu.roll(other, 127, 1), 0.0)
        parts.append((main + moved).astype(BF))
    return jnp.concatenate(parts, axis=1)


def kernel(
    n_chips,
    t_ref,
    ua_ref,
    ub_ref,
    ur_ref,
    sa_ref,
    sb_ref,
    sr_ref,
    bias_ref,
    perm_ref,
    got_ref,
    twin_ref,
    prod,
    image,
    rim_out,
    rim_in,
    chunks,
    rim_send,
    rim_recv,
    send_sem,
    recv_sem,
    own_sem,
    twin_send,
    twin_recv,
):
    n_win = 2 * n_chips
    w = lax.axis_index("win")
    chip, core = w // 2, w % 2
    y, x = chip // SIDE, chip % SIDE
    twin = chip * 2 + 1 - core
    right, left = (w + 1) % n_win, (w + n_win - 1) % n_win
    across = jnp.where(core == 1, right, left)

    barrier = pltpu.get_barrier_semaphore()

    def greet(s, _):
        other = ((chip + s) % n_chips) * 2 + core
        pl.semaphore_signal(barrier, 1, device_id={"win": other}, device_id_type=MESH)
        return 0

    lax.fori_loop(1, n_chips, greet, 0)
    pl.semaphore_signal(barrier, 1, device_id={"win": twin}, device_id_type=MESH)
    pl.semaphore_signal(barrier, 1, device_id={"win": across}, device_id_type=MESH)

    row8 = lax.broadcasted_iota(jnp.int32, (8, 128), 0)

    def columns(zs, j):
        return jnp.concatenate([t_ref[m, z, j] for z in zs for m in range(2)], axis=0)

    def halves(value, v):
        for h in range(2):
            first = value[8 * v : 8 * v + 8, h * 128 : h * 128 + 128]
            second = value[8 * v : 8 * v + 8, 256 + h * 128 : 256 + h * 128 + 128]
            yield h, jnp.where(row8 < 4, first, pltpu.roll(second, 4, 0)), jnp.where(
                row8 < 4, pltpu.roll(first, 4, 0), second
            )

    def rims(zs, w_ref, kinds, channel):
        rhs = jnp.concatenate([columns(zs, 0), columns(zs, 2)], axis=1)
        n = rhs.shape[0]
        rows = kinds * 4
        prod[: 8 * rows, :n] = lax.dot_general(w_ref[...], rhs, NT, preferred_element_type=F32)
        for zi in range(len(zs)):
            value = jnp.dot(
                latitude(prod, rows, zi * 128), perm_ref[...], preferred_element_type=F32
            )
            for v in range(kinds // 2):
                c0, c1 = channel(zi, 2 * v), channel(zi, 2 * v + 1)
                for h, one, two in halves(value, v):
                    rim_out[2 * c0 + h] = one.astype(BF)
                    rim_out[2 * c1 + h] = two.astype(BF)

    def inner(zs, a_ref, b_ref, kinds, channel):
        t01 = [columns(zs, 0), columns(zs, 1)]
        rhs = jnp.concatenate(t01 + [columns(zs, 2)], axis=1)
        n = rhs.shape[0]
        rows = kinds * 8
        prod[: 8 * rows, :n] = lax.dot_general(a_ref[...], rhs, NT, preferred_element_type=F32)
        for zi in range(len(zs)):
            value = jnp.dot(
                latitude(prod, rows, zi * 128), perm_ref[...], preferred_element_type=F32
            )
            for k in range(kinds):
                c = channel(zi, k)
                for m in range(2):
                    for h in range(2):
                        lo = m * 256 + h * 128
                        image[2 * c + h, m] = value[8 * k : 8 * k + 8, lo : lo + 128] + bias_ref[c]
        rhs = jnp.concatenate(t01, axis=1)
        rows = kinds * 4
        prod[: 8 * rows, :n] = lax.dot_general(b_ref[...], rhs, NT, preferred_element_type=F32)
        for zi in range(len(zs)):
            value = jnp.dot(
                latitude(prod, rows, zi * 128), perm_ref[...], preferred_element_type=F32
            )
            for v in range(kinds // 2):
                c0, c1 = channel(zi, 2 * v), channel(zi, 2 * v + 1)
                for h, one, two in halves(value, v):
                    image[2 * c0 + h, 2] = one + bias_ref[c0]
                    image[2 * c1 + h, 2] = two + bias_ref[c1]

    levels = t_ref.shape[1]
    pairs = levels // 2

    def upper_rims(q, _):
        p = pairs - 1 - q
        rims((2 * p, 2 * p + 1), ur_ref, 10, lambda zi, k: 13 * (k // 2) + 2 * (2 * p + zi) + k % 2)
        return 0

    def upper_inner(q, _):
        p = pairs - 1 - q
        inner(
            (2 * p, 2 * p + 1),
            ua_ref,
            ub_ref,
            10,
            lambda zi, k: 13 * (k // 2) + 2 * (2 * p + zi) + k % 2,
        )
        return 0

    def surface_channel(zi, k):
        return VARS_UP * LEVELS + k

    lax.fori_loop(0, pairs, upper_rims, 0)
    rims((levels - 1,), sr_ref, 4, surface_channel)

    pl.semaphore_wait(barrier, n_chips + 1)
    rim_copies = []
    for side, other in ((0, right), (1, left)):
        copy = pltpu.make_async_remote_copy(
            src_ref=rim_out,
            dst_ref=rim_in.at[side],
            send_sem=rim_send.at[side],
            recv_sem=rim_recv.at[side],
            device_id={"win": other},
            device_id_type=MESH,
        )
        copy.start()
        rim_copies.append(copy)

    lax.fori_loop(0, pairs, upper_inner, 0)
    inner((levels - 1,), sa_ref, sb_ref, 4, surface_channel)

    for copy in rim_copies:
        copy.wait()

    def add_rims(q, _):
        for u in range(6):
            t = q * 6 + u
            before = rim_in[0, t].astype(F32)
            after = rim_in[1, t].astype(F32)
            image[t, 2] += jnp.where(row8 % 4 < 2, before, 0.0)
            image[t, 0] += jnp.where(row8 >= 6, pltpu.roll(after, 4, 0), 0.0)
            image[t, 1] += jnp.where(row8 >= 6, after, 0.0)
        return 0

    lax.fori_loop(0, ROWS // 6, add_rims, 0)

    lane = lax.broadcasted_iota(jnp.int32, (8, 128), 1)

    def send_copy(s):
        dy, dx = offset_of(s)
        to = ((y + dy) % SIDE) * SIDE + (x + dx) % SIDE
        return to, pltpu.make_async_remote_copy(
            src_ref=chunks.at[s],
            dst_ref=got_ref.at[s],
            send_sem=send_sem.at[s],
            recv_sem=recv_sem.at[s],
            device_id={"win": to * 2 + core},
            device_id_type=MESH,
        )

    def make_chunk(s, to):
        tails = jnp.zeros((8, 128), F32)
        for k in range(2):
            d = to * 2 + k
            t = (d * ROWS) // 128
            o = (d * ROWS) % 128
            back = (128 - o) % 128
            for g in range(3):
                a = pltpu.roll(image[t, g], back, 1)
                b = pltpu.roll(image[t + 1, g], back, 1)
                c = pltpu.roll(image[t + 2, g], back, 1)
                chunks[s, 4 * k + g] = jnp.where(lane < 128 - o, a, b).astype(BF)
                tail = jnp.where(lane < 128 - o, b, c)
                for slot in (g,) if g < 2 else (2, 3):
                    at = 64 * k + 16 * slot
                    moved = pltpu.roll(tail, at, 1) if at else tail
                    tails = jnp.where((lane >= at) & (lane < at + 10), moved, tails)
        chunks[s, 3] = tails.astype(BF)

    make_chunk(0, chip)
    own = pltpu.make_async_copy(chunks.at[0], got_ref.at[0], own_sem)
    own.start()

    def exchange(s, _):
        to, copy = send_copy(s)
        make_chunk(s, to)
        copy.start()
        return 0

    lax.fori_loop(1, n_chips, exchange, 0)
    own.wait()

    def twin_copy(g):
        part = pl.ds(g * SIDE, SIDE)
        return pltpu.make_async_remote_copy(
            src_ref=got_ref.at[part, pl.ds(3 * (1 - core), 4)],
            dst_ref=twin_ref.at[part],
            send_sem=twin_send.at[g],
            recv_sem=twin_recv.at[g],
            device_id={"win": twin},
            device_id_type=MESH,
        )

    def arrived(s, _):
        send_copy(s)[1].wait_recv()
        return 0

    for g in range(n_chips // SIDE):
        lax.fori_loop(max(1, g * SIDE), (g + 1) * SIDE, arrived, 0)
        twin_copy(g).start()

    def left_here(s, _):
        send_copy(s)[1].wait_send()
        return 0

    lax.fori_loop(1, n_chips, left_here, 0)
    for g in range(n_chips // SIDE):
        twin_copy(g).wait()


def finish(n_chips, got_ref, twin_ref, out_ref):
    w = lax.axis_index("win")
    chip, core = w // 2, w % 2
    y, x = chip // SIDE, chip % SIDE
    first = core == 0
    row = lax.broadcasted_iota(jnp.int32, (8, 128), 0)
    lane = lax.broadcasted_iota(jnp.int32, (8, 128), 1)
    top = row < 4
    spot = lane - 64 * core
    bands = ((spot >= 0) & (spot < 10)) | ((spot >= 16) & (spot < 26))
    third = (spot >= 32) & (spot < 42)
    fourth = (spot >= 48) & (spot < 58)

    def select(mask, value):
        return jnp.where(mask, value, 0.0)

    r = lax.broadcasted_iota(jnp.int32, (2 * ROWS, 384), 0)
    k = lax.broadcasted_iota(jnp.int32, (2 * ROWS, 384), 1)
    rho, m = r // 2, r % 2
    at = 256 + 64 * core + 16 * m + rho - 128
    hot = ((rho < 128) & (k == 128 * m + rho)) | ((rho >= 128) & ((k == at) | (k == at + 32)))
    pick = jnp.where(hot, 1.0, 0.0).astype(BF)

    for block in range(n_chips // 16):
        pieces = []
        for i in range(16):
            p = block * 16 + i
            s = step_of((y - p // SIDE + SIDE) % SIDE, (x - p % SIDE + SIDE) % SIDE)
            mine = [got_ref[s, 3 * core + u].astype(F32) for u in range(4)]
            other = [twin_ref[s, u].astype(F32) for u in range(4)]
            mine = [jnp.where(first, mine[u], mine[(u + 1) % 4]) for u in range(4)]
            other = [jnp.where(first, other[u], other[(u + 1) % 4]) for u in range(4)]
            a = [jnp.where(first, mine[u], other[u]) for u in range(4)]
            b = [jnp.where(first, other[u], mine[u]) for u in range(4)]
            blocks = []
            for mm in range(2):
                ra = pltpu.roll(a[mm], 4, 0)
                if mm == 0:
                    rows = [
                        jnp.where(top, a[2], ra),
                        jnp.where(top, ra, pltpu.roll(b[2], 4, 0)),
                        b[0],
                    ]
                else:
                    rows = [
                        jnp.where(top, pltpu.roll(a[2], 4, 0), ra),
                        jnp.where(top, ra, b[2]),
                        b[1],
                    ]
                blocks.append(jnp.concatenate(rows, axis=0))
            ta, tb = a[3], b[3]
            ra, rb = pltpu.roll(ta, 4, 0), pltpu.roll(tb, 4, 0)
            rows = [
                jnp.where(top, select(third, ta) + select(fourth, ra), select(bands, ra)),
                jnp.where(top, select(bands, ra), select(third, rb) + select(fourth, tb)),
                select(bands, tb),
            ]
            blocks.append(jnp.concatenate(rows, axis=0))
            pieces.append(jnp.concatenate(blocks, axis=1))
        stacked = jnp.concatenate(pieces, axis=0).astype(BF)
        out_ref[:, block * 384 : block * 384 + 384] = lax.dot_general(
            pick, stacked, NT, preferred_element_type=F32
        ).astype(BF)


def interleave():
    k = jnp.arange(512)
    b, m, i = k // 128, (k // 64) % 2, k % 64
    target = m * LAT + 4 * i + b
    return (target[:, None] == jnp.arange(512)[None, :]).astype(BF)


def body(n_chips, tokens, w_upper, w_surface, bias):
    t = jnp.transpose(tokens, (0, 1, 3, 2, 4))
    ua, ub, ur = kernel_weights(w_upper, 10)
    sa, sb, sr = kernel_weights(w_surface, 4)
    vmem = pl.BlockSpec(memory_space=pltpu.VMEM)
    smem = pl.BlockSpec(memory_space=pltpu.SMEM)
    anywhere = pl.BlockSpec(memory_space=pl.ANY)
    dma = pltpu.SemaphoreType.DMA
    got, twin = pl.pallas_call(
        functools.partial(kernel, n_chips),
        out_shape=(
            jax.ShapeDtypeStruct((n_chips, 7, 8, 128), BF),
            jax.ShapeDtypeStruct((n_chips, 4, 8, 128), BF),
        ),
        in_specs=[vmem] * 7 + [smem, vmem],
        out_specs=(anywhere, anywhere),
        scratch_shapes=[
            pltpu.VMEM((640, 256), F32),
            pltpu.VMEM((TILES, 3, 8, 128), F32),
            pltpu.VMEM((TILES, 8, 128), BF),
            pltpu.VMEM((2, TILES, 8, 128), BF),
            pltpu.VMEM((n_chips, 7, 8, 128), BF),
            dma((2,)),
            dma((2,)),
            dma((n_chips,)),
            dma((n_chips,)),
            dma,
            dma((n_chips // SIDE,)),
            dma((n_chips // SIDE,)),
        ],
        compiler_params=pltpu.CompilerParams(
            collective_id=0, has_side_effects=True, vmem_limit_bytes=40 * 2**20
        ),
        name="recover",
    )(t, ua, ub, ur, sa, sb, sr, bias, interleave())
    rows = pl.pallas_call(
        functools.partial(finish, n_chips),
        out_shape=jax.ShapeDtypeStruct((2 * ROWS, n_chips * 24), BF),
        in_specs=[vmem, vmem],
        out_specs=vmem,
        compiler_params=pltpu.CompilerParams(vmem_limit_bytes=40 * 2**20),
        name="finish",
    )(got, twin)
    return jnp.transpose(rows.reshape(ROWS, 2, n_chips * 24), (1, 0, 2))


def solution(mesh):
    n_chips = mesh.shape["win"] // 2
    return jax.shard_map(
        functools.partial(body, n_chips),
        mesh=mesh,
        in_specs=(P("grp", None, None, "win", None), P(), P(), P()),
        out_specs=P("grp", "win", None),
        check_vma=False,
    )
```

time: 208 us -> 70.6 us (0.34)
  local copies, waits for them, and re-layouts: 97.5 us -> 6.86 us
  Pallas kernels: 0 us -> 61.9 us
  blocking collectives: 57.9 us -> 0 us
  starting transfers between devices: 20.7 us -> 0 us
  other arithmetic: 20 us -> 1.36 us
  matrix products: 8.92 us -> 0 us
    pallas_call x0 -> x2, Pallas kernels: none -> 61.9 us  [the longest x1 61 us: body(): pl.pallas_call(functools.partial(kernel, n_chips), out_shape=(jax.ShapeDt...]
    all_to_all x2 -> x0, blocking collectives: 57.9 us -> none  [moved_by_axis(): result = lax.all_to_all(result, axes[k], k, k, tiled=True)]
    reshape x5, local copies, waits for them, and re-layouts: 45.5 us -> 1.83 us  [the longest x1 1.5 us: body(): return jnp.transpose(rows.reshape(ROWS, 2, n_chips * 24), (1, 0, 2))]
    transpose x4 -> x0, local copies, waits for them, and re-layouts: 38.1 us -> none  [the longest x2 32.3 us: latitude_add(): return jnp.swapaxes(summed, -1, -2)]
    ppermute x2 -> x0, starting transfers between devices: 20.7 us -> none  [shifted(): return lax.ppermute(x, axis, [(i, (i + by) % size) for i in range(size)])]
    squeeze x2 -> x0, other arithmetic: 12.2 us -> none  [latitude_add(): first = values[..., 0, :, :]]
    dot_general x2 -> x0, matrix products: 8.92 us -> none  [the longest x1 7.48 us: project(): jnp.einsum('dvlpqrs,mzjdi->vlpqrsmzji', kernel_up, upper_tok, preferred_e...]
    squeeze x2 -> x0, local copies, waits for them, and re-layouts: 8.78 us -> none  [intersection_add(): first = lax.index_in_dim(values, 0, axis + 1, keepdims=False)]
  transfers between devices with their start and end apart: 2 -> 0, of which waited for: 2 -> 0; matrix products, arithmetic and copies ran while one was open for 0% -> 0% of each run, Pallas kernels for 0% -> 0%
where the time goes in v1:
time: 70.6 us; the launch traced here: 70.4 us
  Pallas kernels  61.9 us (88%)
  local copies, waits for them, and re-layouts  6.86 us (10%)
  other arithmetic  1.36 us (2%)
    pallas_call x1, Pallas kernels, body(): pl.pallas_call(functools.partial(kernel, n_chips), out_shape=(jax.ShapeDt...  61 us
    unnamed x8, local copies, waits for them, and re-layouts  3.5 us
    reshape x1, local copies, waits for them, and re-layouts, body(): return jnp.transpose(rows.reshape(ROWS, 2, n_chips * 24), (1, 0, 2))  1.5 us

profile of v1, /device:TPU:513, one launch (start us, length us, event | category | flops | bytes accessed | tf_op | source)
XLA Modules:
  0.0 70.4 jit_solution(16792573647028309058)
XLA Ops:
  0.0 1.1 %copy.11 = bf16[384,256]{0,1:T(8,128)(2,1)S(1)} copy(bf16[384,256]{1,0:T(8,128)(2,1)} %param.6) | data formatting | bytes 393216 | tf_op args[2]
  1.1 0.1 slice.52
  1.2 0.1 fusion.32
  1.2 0.1 pad.50
  1.3 0.2 fusion.16
  1.5 0.1 copy.14
  1.6 0.1 reshape.77.sr_ref
  1.6 0.1 copy.13
  1.7 0.1 reshape.76.sb_ref
  1.8 0.0 copy-start.2
  1.8 0.1 fusion.33
  1.8 0.1 fusion.13
  2.0 0.8 %copy-done.2 = bf16[384,640]{1,0:T(8,128)(2,1)S(1)} copy-done((bf16[384,640]{1,0:T(8,128)(2,1)S(1)}, bf16[384,640]{1,0:T(8,128)(2,1)}, u32[]{:S(2)}) %copy-start.2) | copy-done | bytes 491544
  2.8 0.3 copy.7
  3.1 0.1 slice.47
  3.2 0.2 fusion.30
  3.4 0.2 pad.45
  3.5 0.5 fusion.14
  4.1 0.2 copy.10
  4.3 0.1 reshape.73.ur_ref
  4.4 0.2 copy.9
  4.6 0.1 reshape.72.ub_ref
  4.7 0.2 fusion.31
  4.9 0.4 fusion.5
  5.2 0.0 copy-start
  5.3 0.0 copy-start.1
  5.3 0.1 copy.8
  5.4 0.2 fusion.10.perm_ref
  5.5 1.4 %copy-done = bf16[2,8,64,3,384]{4,2,3,1,0:T(8,128)(2,1)S(1)} copy-done((bf16[2,8,64,3,384]{4,2,3,1,0:T(8,128)(2,1)S(1)}, bf16[2,8,64,3,384]{4,2,3,1,0:T(8,128)(2,1)}, u32[]{:S(2)}) %copy-start) | copy-done | bytes 2359320
  6.9 0.0 copy-done.1
  6.9 61.0 %recover.1 = (bf16[64,7,8,128]{3,2,1,0:T(8,128)(2,1)S(1)}, bf16[64,4,8,128]{3,2,1,0:T(8,128)(2,1)S(1)}) custom-call(bf16[2,8,3,64,384]{4,3,2,1,0:T(8,128)(2,1)S(1)} %bitcast.12, bf16[640,1152]{1,0:T(8,128)(2,1)S(1)} %bitcast.10, bf16[320,768]{1,0:T(8,128)(2,1)S(1)} %reshape.72.ub_ref, bf16[320,768]{1,0:T(8,128)(2,1)S(1)} %reshape.73.ur_ref, ...), custom_call_target="tpu_custom_call" | custom-call | tf_op jit(solution)/shard_map/recover/pallas_call | solution.py:377
  68.0 0.9 %finish.1 = bf16[276,1536]{1,0:T(8,128)(2,1)S(1)} custom-call(bf16[64,7,8,128]{3,2,1,0:T(8,128)(2,1)S(1)} %get-tuple-element.7.got_ref, bf16[64,4,8,128]{3,2,1,0:T(8,128)(2,1)S(1)} %get-tuple-element.8.twin_ref), custom_call_target="tpu_custom_call" | custom-call | tf_op jit(solution)/shard_map/finish/pallas_call | solution.py:404
  68.9 1.5 %reshape.78 = bf16[138,2,1536]{2,1,0:T(2,128)(2,1)} reshape(bf16[276,1536]{1,0:T(8,128)(2,1)S(1)} %finish.1) | data formatting | bytes 1695744 | tf_op jit(solution)/shard_map/reshape | solution.py:412
  (2 shorter events, 0.1 us)
Async XLA Ops:
  1.8 1.0 %copy-start.2 = (bf16[384,640]{1,0:T(8,128)(2,1)S(1)}, bf16[384,640]{1,0:T(8,128)(2,1)}, u32[]{:S(2)}) copy-start(bf16[384,640]{1,0:T(8,128)(2,1)} %param.5) | copy-start | bytes 1474564
  5.2 1.7 %copy-start = (bf16[2,8,64,3,384]{4,2,3,1,0:T(8,128)(2,1)S(1)}, bf16[2,8,64,3,384]{4,2,3,1,0:T(8,128)(2,1)}, u32[]{:S(2)}) copy-start(bf16[2,8,64,3,384]{4,2,3,1,0:T(8,128)(2,1)} %param.4) | copy-start | bytes 7077892
  5.3 1.7 %copy-start.1 = (f32[69]{0:T(128)S(1)}, f32[69]{0:T(128)}, u32[]{:S(2)}) copy-start(f32[69]{0:T(128)} %bias_ref.1) | copy-start | bytes 832

commit v2 on v1

--- a/solution.py
+++ b/solution.py
@@ -30,51 +30,92 @@
     return (s // SIDE + dx) % SIDE, dx
 
 
-def kernel_weights(w, kinds):
-    width = w.shape[0]
-    wt = jnp.transpose(w.reshape(width, kinds, 8, 8), (2, 1, 3, 0))
-
-    def rows(lo, hi, before, after):
-        return jnp.pad(wt[:, :, lo:hi], ((0, 0), (0, 0), (before, after), (0, 0)))
-
-    def join(*parts):
-        return jnp.concatenate(parts, -1).reshape(-1, width * len(parts))
-
-    last = join(rows(6, 8, 0, 6), rows(2, 8, 0, 2), rows(0, 6, 2, 0))
-    first = join(rows(2, 6, 0, 0), rows(0, 2, 2, 0))
-    rims = join(rows(0, 2, 2, 0), rows(6, 8, 0, 2))
-    return last, first, rims
-
-
-def latitude(product_ref, kinds_rows, lane0):
-    lane = lax.broadcasted_iota(jnp.int32, (1, 128), 1) % 64
+def prepare(w_ref, kinds, last_ref, first_ref, rims_ref):
+    width = w_ref.shape[0]
+    row = lax.broadcasted_iota(jnp.int32, (8, width), 0)
+    a = lax.broadcasted_iota(jnp.int32, (128, 128), 0)
+    b = lax.broadcasted_iota(jnp.int32, (128, 128), 1)
+    unit = jnp.where(a == b, 1.0, 0.0).astype(BF)
+
+    def keep(mask, value):
+        return jnp.where(mask, value, 0.0)
+
+    turned = [
+        lax.dot_general(unit, w_ref[:, i * 128 : i * 128 + 128], NT, preferred_element_type=F32)
+        for i in range(kinds // 2)
+    ]
+    for pair in range(kinds // 2):
+        for lat in range(8):
+            down, up = [], []
+            for k in range(2):
+                eight = turned[pair][k * 64 + lat * 8 : k * 64 + lat * 8 + 8]
+                down.append(pltpu.roll(eight, 2, 0))
+                up.append(pltpu.roll(eight, 6, 0))
+            at = (lat * kinds + 2 * pair) * 8
+            parts = [
+                [keep(row < 2, down[k]), keep(row < 6, up[k]), keep(row >= 2, down[k])]
+                for k in range(2)
+            ]
+            for j in range(3):
+                both = jnp.concatenate([parts[0][j], parts[1][j]], axis=0)
+                last_ref[at : at + 16, j * width : (j + 1) * width] = both.astype(BF)
+            half = at // 2
+            outer = keep((row == 2) | (row == 3), down[0]) + keep(row >= 6, up[1])
+            middle = jnp.where(row < 4, up[0], down[1])
+            first_ref[half : half + 8, :width] = middle.astype(BF)
+            first_ref[half : half + 8, width:] = outer.astype(BF)
+            tail = keep(row < 2, down[0]) + keep((row == 4) | (row == 5), up[1])
+            rims_ref[half : half + 8, :width] = outer.astype(BF)
+            rims_ref[half : half + 8, width:] = tail.astype(BF)
+
+
+def latitude(product_ref, rows, lane0):
+    place = lax.broadcasted_iota(jnp.int32, (rows, 128), 1)
+    lane = place % 64
     parts = []
     for b in range(4):
-        main = product_ref[(b + 2) * kinds_rows : (b + 3) * kinds_rows, lane0 : lane0 + 128]
+        main = product_ref[(b + 2) * rows : (b + 3) * rows, lane0 : lane0 + 128]
         a = (b + 6) % 8
-        other = product_ref[a * kinds_rows : (a + 1) * kinds_rows, lane0 : lane0 + 128]
+        other = product_ref[a * rows : (a + 1) * rows, lane0 : lane0 + 128]
         if b < 2:
             moved = jnp.where(lane != 0, pltpu.roll(other, 1, 1), 0.0)
         else:
             moved = jnp.where(lane != 63, pltpu.roll(other, 127, 1), 0.0)
-        parts.append((main + moved).astype(BF))
-    return jnp.concatenate(parts, axis=1)
+        parts.append(main + moved)
+    low = place < 64
+    turned = [pltpu.roll(p, 64, 1) for p in parts]
+    return [
+        jnp.concatenate(
+            [jnp.where(low, parts[0], turned[1]), jnp.where(low, parts[2], turned[3])], axis=1
+        ),
+        jnp.concatenate(
+            [jnp.where(low, turned[0], parts[1]), jnp.where(low, turned[2], parts[3])], axis=1
+        ),
+    ]
 
 
 def kernel(
     n_chips,
     t_ref,
+    wu_any,
+    ws_any,
+    bias_ref,
+    out_ref,
+    got_ref,
+    twin_ref,
+    held,
+    wu_ref,
+    ws_ref,
     ua_ref,
     ub_ref,
     ur_ref,
     sa_ref,
     sb_ref,
     sr_ref,
-    bias_ref,
     perm_ref,
-    got_ref,
-    twin_ref,
-    prod,
+    prod_a,
+    prod_b,
+    token_sem,
     image,
     rim_out,
     rim_in,
@@ -83,7 +124,6 @@
     rim_recv,
     send_sem,
     recv_sem,
-    own_sem,
     twin_send,
     twin_recv,
 ):
@@ -95,6 +135,21 @@
     right, left = (w + 1) % n_win, (w + n_win - 1) % n_win
     across = jnp.where(core == 1, right, left)
 
+    levels = t_ref.shape[1]
+    pairs = levels // 2
+
+    def token_copy(z):
+        return pltpu.make_async_copy(t_ref.at[:, z], held.at[:, z], token_sem.at[z])
+
+    weight_copies = [
+        pltpu.make_async_copy(wu_any, wu_ref, token_sem.at[levels]),
+        pltpu.make_async_copy(ws_any, ws_ref, token_sem.at[levels + 1]),
+    ]
+    for copy in weight_copies:
+        copy.start()
+    for z in range(levels - 1, -1, -1):
+        token_copy(z).start()
+
     barrier = pltpu.get_barrier_semaphore()
 
     def greet(s, _):
@@ -106,31 +161,50 @@
     pl.semaphore_signal(barrier, 1, device_id={"win": twin}, device_id_type=MESH)
     pl.semaphore_signal(barrier, 1, device_id={"win": across}, device_id_type=MESH)
 
+    k256 = lax.broadcasted_iota(jnp.int32, (LAT, LAT), 0)
+    n256 = lax.broadcasted_iota(jnp.int32, (LAT, LAT), 1)
+    perm_ref[...] = jnp.where(4 * (k256 % 64) + k256 // 64 == n256, 1.0, 0.0).astype(BF)
+    weight_copies[0].wait()
+    prepare(wu_ref, 2 * VARS_UP, ua_ref, ub_ref, ur_ref)
+    weight_copies[1].wait()
+    prepare(ws_ref, VARS_SF, sa_ref, sb_ref, sr_ref)
+
     row8 = lax.broadcasted_iota(jnp.int32, (8, 128), 0)
 
     def columns(zs, j):
-        return jnp.concatenate([t_ref[m, z, j] for z in zs for m in range(2)], axis=0)
-
-    def halves(value, v):
+        return jnp.concatenate([held[m, z, j] for z in zs for m in range(2)], axis=0)
+
+    def halves(values, at):
         for h in range(2):
-            first = value[8 * v : 8 * v + 8, h * 128 : h * 128 + 128]
-            second = value[8 * v : 8 * v + 8, 256 + h * 128 : 256 + h * 128 + 128]
+            first = values[0][at : at + 8, h * 128 : h * 128 + 128]
+            second = values[1][at : at + 8, h * 128 : h * 128 + 128]
             yield h, jnp.where(row8 < 4, first, pltpu.roll(second, 4, 0)), jnp.where(
                 row8 < 4, pltpu.roll(first, 4, 0), second
             )
+
+    def interleaved(blocks):
+        stacked = jnp.concatenate([b.astype(BF) for b in blocks], axis=0)
+        value = jnp.dot(stacked, perm_ref[...], preferred_element_type=F32)
+        out, at = [], 0
+        for b in blocks:
+            out.append(value[at : at + b.shape[0]])
+            at += b.shape[0]
+        return out
+
+    def per_member(product_ref, rows, count):
+        found = [latitude(product_ref, rows, zi * 128) for zi in range(count)]
+        return [jnp.concatenate([f[m] for f in found], axis=0) for m in range(2)]
 
     def rims(zs, w_ref, kinds, channel):
         rhs = jnp.concatenate([columns(zs, 0), columns(zs, 2)], axis=1)
         n = rhs.shape[0]
         rows = kinds * 4
-        prod[: 8 * rows, :n] = lax.dot_general(w_ref[...], rhs, NT, preferred_element_type=F32)
+        prod_b[: 8 * rows, :n] = lax.dot_general(w_ref[...], rhs, NT, preferred_element_type=F32)
+        values = interleaved(per_member(prod_b, rows, len(zs)))
         for zi in range(len(zs)):
-            value = jnp.dot(
-                latitude(prod, rows, zi * 128), perm_ref[...], preferred_element_type=F32
-            )
             for v in range(kinds // 2):
                 c0, c1 = channel(zi, 2 * v), channel(zi, 2 * v + 1)
-                for h, one, two in halves(value, v):
+                for h, one, two in halves(values, zi * rows + 8 * v):
                     rim_out[2 * c0 + h] = one.astype(BF)
                     rim_out[2 * c1 + h] = two.astype(BF)
 
@@ -138,36 +212,31 @@
         t01 = [columns(zs, 0), columns(zs, 1)]
         rhs = jnp.concatenate(t01 + [columns(zs, 2)], axis=1)
         n = rhs.shape[0]
-        rows = kinds * 8
-        prod[: 8 * rows, :n] = lax.dot_general(a_ref[...], rhs, NT, preferred_element_type=F32)
+        rows_a, rows_b = kinds * 8, kinds * 4
+        prod_a[: 8 * rows_a, :n] = lax.dot_general(a_ref[...], rhs, NT, preferred_element_type=F32)
+        rhs = jnp.concatenate(t01, axis=1)
+        prod_b[: 8 * rows_b, :n] = lax.dot_general(b_ref[...], rhs, NT, preferred_element_type=F32)
+        values = interleaved(
+            per_member(prod_a, rows_a, len(zs)) + per_member(prod_b, rows_b, len(zs))
+        )
         for zi in range(len(zs)):
-            value = jnp.dot(
-                latitude(prod, rows, zi * 128), perm_ref[...], preferred_element_type=F32
-            )
             for k in range(kinds):
                 c = channel(zi, k)
+                at = zi * rows_a + 8 * k
                 for m in range(2):
                     for h in range(2):
-                        lo = m * 256 + h * 128
-                        image[2 * c + h, m] = value[8 * k : 8 * k + 8, lo : lo + 128] + bias_ref[c]
-        rhs = jnp.concatenate(t01, axis=1)
-        rows = kinds * 4
-        prod[: 8 * rows, :n] = lax.dot_general(b_ref[...], rhs, NT, preferred_element_type=F32)
-        for zi in range(len(zs)):
-            value = jnp.dot(
-                latitude(prod, rows, zi * 128), perm_ref[...], preferred_element_type=F32
-            )
+                        lo = h * 128
+                        image[2 * c + h, m] = values[m][at : at + 8, lo : lo + 128] + bias_ref[c]
             for v in range(kinds // 2):
                 c0, c1 = channel(zi, 2 * v), channel(zi, 2 * v + 1)
-                for h, one, two in halves(value, v):
+                for h, one, two in halves(values[2:], zi * rows_b + 8 * v):
                     image[2 * c0 + h, 2] = one + bias_ref[c0]
                     image[2 * c1 + h, 2] = two + bias_ref[c1]
 
-    levels = t_ref.shape[1]
-    pairs = levels // 2
-
     def upper_rims(q, _):
         p = pairs - 1 - q
+        token_copy(2 * p + 1).wait()
+        token_copy(2 * p).wait()
         rims((2 * p, 2 * p + 1), ur_ref, 10, lambda zi, k: 13 * (k // 2) + 2 * (2 * p + zi) + k % 2)
         return 0
 
@@ -188,6 +257,12 @@
     lax.fori_loop(0, pairs, upper_rims, 0)
     rims((levels - 1,), sr_ref, 4, surface_channel)
 
+    def all_inner():
+        lax.fori_loop(0, pairs, upper_inner, 0)
+        inner((levels - 1,), sa_ref, sb_ref, 4, surface_channel)
+
+    late = (y >= SIDE // 2) | (chip == 0)
+    pl.when(jnp.logical_not(late))(all_inner)
     pl.semaphore_wait(barrier, n_chips + 1)
     rim_copies = []
     for side, other in ((0, right), (1, left)):
@@ -202,8 +277,7 @@
         copy.start()
         rim_copies.append(copy)
 
-    lax.fori_loop(0, pairs, upper_inner, 0)
-    inner((levels - 1,), sa_ref, sb_ref, 4, surface_channel)
+    pl.when(late)(all_inner)
 
     for copy in rim_copies:
         copy.wait()
@@ -254,18 +328,17 @@
         chunks[s, 3] = tails.astype(BF)
 
     make_chunk(0, chip)
-    own = pltpu.make_async_copy(chunks.at[0], got_ref.at[0], own_sem)
-    own.start()
-
-    def exchange(s, _):
-        to, copy = send_copy(s)
-        make_chunk(s, to)
-        copy.start()
-        return 0
-
-    lax.fori_loop(1, n_chips, exchange, 0)
-    own.wait()
-
+    got_ref[0] = chunks[0]
+
+    def exchange(q, _):
+        for u in range(3):
+            s = 1 + q * 3 + u
+            to, copy = send_copy(s)
+            make_chunk(s, to)
+            copy.start()
+        return 0
+
+    lax.fori_loop(0, (n_chips - 1) // 3, exchange, 0)
     def twin_copy(g):
         part = pl.ds(g * SIDE, SIDE)
         return pltpu.make_async_remote_copy(
@@ -292,12 +365,10 @@
     lax.fori_loop(1, n_chips, left_here, 0)
     for g in range(n_chips // SIDE):
         twin_copy(g).wait()
-
-
-def finish(n_chips, got_ref, twin_ref, out_ref):
-    w = lax.axis_index("win")
-    chip, core = w // 2, w % 2
-    y, x = chip // SIDE, chip % SIDE
+    finish(n_chips, y, x, core, got_ref, twin_ref, out_ref)
+
+
+def finish(n_chips, y, x, core, got_ref, twin_ref, out_ref):
     first = core == 0
     row = lax.broadcasted_iota(jnp.int32, (8, 128), 0)
     lane = lax.broadcasted_iota(jnp.int32, (8, 128), 1)
@@ -354,36 +425,41 @@
             blocks.append(jnp.concatenate(rows, axis=0))
             pieces.append(jnp.concatenate(blocks, axis=1))
         stacked = jnp.concatenate(pieces, axis=0).astype(BF)
-        out_ref[:, block * 384 : block * 384 + 384] = lax.dot_general(
-            pick, stacked, NT, preferred_element_type=F32
-        ).astype(BF)
-
-
-def interleave():
-    k = jnp.arange(512)
-    b, m, i = k // 128, (k // 64) % 2, k % 64
-    target = m * LAT + 4 * i + b
-    return (target[:, None] == jnp.arange(512)[None, :]).astype(BF)
+        out_ref[:, :, block * 384 : block * 384 + 384] = (
+            lax.dot_general(pick, stacked, NT, preferred_element_type=F32)
+            .astype(BF)
+            .reshape(ROWS, 2, 384)
+        )
 
 
 def body(n_chips, tokens, w_upper, w_surface, bias):
     t = jnp.transpose(tokens, (0, 1, 3, 2, 4))
-    ua, ub, ur = kernel_weights(w_upper, 10)
-    sa, sb, sr = kernel_weights(w_surface, 4)
+    width = t.shape[-1]
     vmem = pl.BlockSpec(memory_space=pltpu.VMEM)
     smem = pl.BlockSpec(memory_space=pltpu.SMEM)
-    anywhere = pl.BlockSpec(memory_space=pl.ANY)
+    hbm = pl.BlockSpec(memory_space=pl.ANY)
     dma = pltpu.SemaphoreType.DMA
-    got, twin = pl.pallas_call(
+    rows = pl.pallas_call(
         functools.partial(kernel, n_chips),
-        out_shape=(
-            jax.ShapeDtypeStruct((n_chips, 7, 8, 128), BF),
-            jax.ShapeDtypeStruct((n_chips, 4, 8, 128), BF),
-        ),
-        in_specs=[vmem] * 7 + [smem, vmem],
-        out_specs=(anywhere, anywhere),
+        out_shape=jax.ShapeDtypeStruct((ROWS, 2, n_chips * 24), BF),
+        in_specs=[hbm, hbm, hbm, smem],
+        out_specs=vmem,
         scratch_shapes=[
+            pltpu.VMEM((n_chips, 7, 8, 128), BF),
+            pltpu.VMEM((n_chips, 4, 8, 128), BF),
+            pltpu.VMEM(t.shape, BF),
+            pltpu.VMEM(w_upper.shape, BF),
+            pltpu.VMEM(w_surface.shape, BF),
+            pltpu.VMEM((640, 3 * width), BF),
+            pltpu.VMEM((320, 2 * width), BF),
+            pltpu.VMEM((320, 2 * width), BF),
+            pltpu.VMEM((256, 3 * width), BF),
+            pltpu.VMEM((128, 2 * width), BF),
+            pltpu.VMEM((128, 2 * width), BF),
+            pltpu.VMEM((LAT, LAT), BF),
             pltpu.VMEM((640, 256), F32),
+            pltpu.VMEM((320, 256), F32),
+            dma((t.shape[1] + 2,)),
             pltpu.VMEM((TILES, 3, 8, 128), F32),
             pltpu.VMEM((TILES, 8, 128), BF),
             pltpu.VMEM((2, TILES, 8, 128), BF),
@@ -392,24 +468,15 @@
             dma((2,)),
             dma((n_chips,)),
             dma((n_chips,)),
-            dma,
             dma((n_chips // SIDE,)),
             dma((n_chips // SIDE,)),
         ],
         compiler_params=pltpu.CompilerParams(
-            collective_id=0, has_side_effects=True, vmem_limit_bytes=40 * 2**20
+            collective_id=0, has_side_effects=True, vmem_limit_bytes=64 * 10**6
         ),
         name="recover",
-    )(t, ua, ub, ur, sa, sb, sr, bias, interleave())
-    rows = pl.pallas_call(
-        functools.partial(finish, n_chips),
-        out_shape=jax.ShapeDtypeStruct((2 * ROWS, n_chips * 24), BF),
-        in_specs=[vmem, vmem],
-        out_specs=vmem,
-        compiler_params=pltpu.CompilerParams(vmem_limit_bytes=40 * 2**20),
-        name="finish",
-    )(got, twin)
-    return jnp.transpose(rows.reshape(ROWS, 2, n_chips * 24), (1, 0, 2))
+    )(t, w_upper, w_surface, bias)
+    return jnp.transpose(rows, (1, 0, 2))
 
 
 def solution(mesh):

time: 70.6 us -> 65.5 us (0.928)
  local copies, waits for them, and re-layouts: 6.86 us -> 2.64 us
  other arithmetic: 1.36 us -> 0 us
  Pallas kernels: 61.9 us -> 62.7 us
    reshape x5 -> x0, local copies, waits for them, and re-layouts: 1.83 us -> none  [the longest x1 1.5 us: body(): return jnp.transpose(rows.reshape(ROWS, 2, n_chips * 24), (1, 0, 2))]
    concatenate x4 -> x0, other arithmetic: 1.2 us -> none  [join(): return jnp.concatenate(parts, -1).reshape(-1, width * len(parts))]
    unnamed x8 -> x1, local copies, waits for them, and re-layouts: 3.5 us -> 2.64 us
    pallas_call x2 -> x1, Pallas kernels: 61.9 us -> 62.7 us  [body(): pl.pallas_call(functools.partial(kernel, n_chips), out_shape=jax.ShapeDty...]
where the time goes in v2:
time: 65.5 us; the launch traced here: 65.3 us
  Pallas kernels  62.7 us (96%)
  local copies, waits for them, and re-layouts  2.64 us (4%)
    pallas_call x1, Pallas kernels, body(): pl.pallas_call(functools.partial(kernel, n_chips), out_shape=jax.ShapeDty...  62.7 us
    unnamed x1, local copies, waits for them, and re-layouts  2.64 us

profile of v2, /device:TPU:513, one launch (start us, length us, event | category | flops | bytes accessed | tf_op | source)
XLA Modules:
  0.0 65.3 jit_solution(2443487464730863891)
XLA Ops:
  0.0 62.7 %recover.1 = bf16[138,2,1536]{2,1,0:T(2,128)(2,1)} custom-call(bf16[2,8,3,64,384]{4,3,2,1,0:T(8,128)(2,1)} %bitcast.3, bf16[384,640]{1,0:T(8,128)(2,1)} %wu_any.1, bf16[384,256]{1,0:T(8,128)(2,1)} %ws_any.1, f32[69]{0:T(128)} %bias_ref.1), custom_call_target="tpu_custom_call" | custom-call | tf_op jit(solution)/shard_map/recover/pallas_call | solution.py:442
  62.7 2.6 %copy.6 = bf16[2,138,1536]{2,0,1:T(2,128)(2,1)} copy(bf16[2,138,1536]{2,0,1:T(2,128)(2,1)} %bitcast.2) | data formatting | bytes 1695744

commit v3 on v2

--- a/solution.py
+++ b/solution.py
@@ -46,24 +46,25 @@
     ]
     for pair in range(kinds // 2):
         for lat in range(8):
-            down, up = [], []
-            for k in range(2):
-                eight = turned[pair][k * 64 + lat * 8 : k * 64 + lat * 8 + 8]
-                down.append(pltpu.roll(eight, 2, 0))
-                up.append(pltpu.roll(eight, 6, 0))
+            eights = [turned[pair][k * 64 + lat * 8 : k * 64 + lat * 8 + 8] for k in range(2)]
+            across = [pltpu.roll(e, 4, 0) for e in eights]
+            down = [pltpu.roll(e, 2, 0) for e in eights]
+            up = [pltpu.roll(e, 6, 0) for e in eights]
             at = (lat * kinds + 2 * pair) * 8
-            parts = [
-                [keep(row < 2, down[k]), keep(row < 6, up[k]), keep(row >= 2, down[k])]
-                for k in range(2)
-            ]
-            for j in range(3):
-                both = jnp.concatenate([parts[0][j], parts[1][j]], axis=0)
+            for j, parts in enumerate(
+                (
+                    [keep(row < 4, e) for e in across],
+                    eights,
+                    [keep(row >= 4, e) for e in across],
+                )
+            ):
+                both = jnp.concatenate(parts, axis=0)
                 last_ref[at : at + 16, j * width : (j + 1) * width] = both.astype(BF)
             half = at // 2
+            middle = jnp.where(row < 4, up[0], down[1])
+            first_ref[half : half + 8, :width] = keep(row % 4 < 2, middle).astype(BF)
+            first_ref[half : half + 8, width:] = keep(row % 4 >= 2, middle).astype(BF)
             outer = keep((row == 2) | (row == 3), down[0]) + keep(row >= 6, up[1])
-            middle = jnp.where(row < 4, up[0], down[1])
-            first_ref[half : half + 8, :width] = middle.astype(BF)
-            first_ref[half : half + 8, width:] = outer.astype(BF)
             tail = keep(row < 2, down[0]) + keep((row == 4) | (row == 5), up[1])
             rims_ref[half : half + 8, :width] = outer.astype(BF)
             rims_ref[half : half + 8, width:] = tail.astype(BF)
@@ -100,7 +101,6 @@
     wu_any,
     ws_any,
     bias_ref,
-    out_ref,
     got_ref,
     twin_ref,
     held,
@@ -122,6 +122,7 @@
     chunks,
     rim_send,
     rim_recv,
+    own_sem,
     send_sem,
     recv_sem,
     twin_send,
@@ -170,6 +171,7 @@
     prepare(ws_ref, VARS_SF, sa_ref, sb_ref, sr_ref)
 
     row8 = lax.broadcasted_iota(jnp.int32, (8, 128), 0)
+    low4 = row8 % 4 < 2
 
     def columns(zs, j):
         return jnp.concatenate([held[m, z, j] for z in zs for m in range(2)], axis=0)
@@ -204,17 +206,18 @@
         for zi in range(len(zs)):
             for v in range(kinds // 2):
                 c0, c1 = channel(zi, 2 * v), channel(zi, 2 * v + 1)
-                for h, one, two in halves(values, zi * rows + 8 * v):
-                    rim_out[2 * c0 + h] = one.astype(BF)
-                    rim_out[2 * c1 + h] = two.astype(BF)
+                (_, one0, two0), (_, one1, two1) = halves(values, zi * rows + 8 * v)
+                for c, first, second in ((c0, one0, one1), (c1, two0, two1)):
+                    rim_out[0, c] = jnp.where(low4, first, pltpu.roll(second, 2, 0)).astype(BF)
+                    rim_out[1, c] = jnp.where(low4, pltpu.roll(first, 6, 0), second).astype(BF)
 
     def inner(zs, a_ref, b_ref, kinds, channel):
-        t01 = [columns(zs, 0), columns(zs, 1)]
-        rhs = jnp.concatenate(t01 + [columns(zs, 2)], axis=1)
+        three = [columns(zs, j) for j in range(3)]
+        rhs = jnp.concatenate(three, axis=1)
         n = rhs.shape[0]
         rows_a, rows_b = kinds * 8, kinds * 4
         prod_a[: 8 * rows_a, :n] = lax.dot_general(a_ref[...], rhs, NT, preferred_element_type=F32)
-        rhs = jnp.concatenate(t01, axis=1)
+        rhs = jnp.concatenate([three[0], three[2]], axis=1)
         prod_b[: 8 * rows_b, :n] = lax.dot_general(b_ref[...], rhs, NT, preferred_element_type=F32)
         values = interleaved(
             per_member(prod_a, rows_a, len(zs)) + per_member(prod_b, rows_b, len(zs))
@@ -257,17 +260,79 @@
     lax.fori_loop(0, pairs, upper_rims, 0)
     rims((levels - 1,), sr_ref, 4, surface_channel)
 
+    lane = lax.broadcasted_iota(jnp.int32, (8, 128), 1)
+    parts = (pl.ds(0, 4), pl.ds(4, 3))
+
+    def target(s):
+        dy, dx = offset_of(s)
+        return ((y + dy) % SIDE) * SIDE + (x + dx) % SIDE
+
+    def send_copy(half, s):
+        return pltpu.make_async_remote_copy(
+            src_ref=chunks.at[s, parts[half]],
+            dst_ref=got_ref.at[s, parts[half]],
+            send_sem=send_sem.at[half, s],
+            recv_sem=recv_sem.at[half, s],
+            device_id={"win": target(s) * 2 + core},
+            device_id_type=MESH,
+        )
+
+    def window(to, k):
+        d = to * 2 + k
+        o = (d * ROWS) % 128
+        return (d * ROWS) // 128, o, (128 - o) % 128
+
+    def first_part(s):
+        to = target(s)
+        for k in range(2):
+            t, o, back = window(to, k)
+            for g in range(2):
+                a = pltpu.roll(image[t, g], back, 1)
+                b = pltpu.roll(image[t + 1, g], back, 1)
+                chunks[s, 2 * k + g] = jnp.where(lane < 128 - o, a, b).astype(BF)
+
+    def second_part(s):
+        to = target(s)
+        tails = jnp.zeros((8, 128), F32)
+        for k in range(2):
+            t, o, back = window(to, k)
+            a = pltpu.roll(image[t, 2], back, 1)
+            b = pltpu.roll(image[t + 1, 2], back, 1)
+            chunks[s, 4 + 2 * k] = jnp.where(lane < 128 - o, a, b).astype(BF)
+            for slot, g in enumerate((0, 1, 2, 2)):
+                at = 64 * k + 16 * slot
+                b = pltpu.roll(image[t + 1, g], (back + at) % 128, 1)
+                c = pltpu.roll(image[t + 2, g], (back + at) % 128, 1)
+                tail = jnp.where(lane < 128 - o + at, b, c)
+                tails = jnp.where((lane >= at) & (lane < at + 10), tail, tails)
+        chunks[s, 5] = tails.astype(BF)
+
+    def own_copy(half):
+        return pltpu.make_async_copy(
+            chunks.at[0, parts[half]], got_ref.at[0, parts[half]], own_sem.at[half]
+        )
+
     def all_inner():
         lax.fori_loop(0, pairs, upper_inner, 0)
         inner((levels - 1,), sa_ref, sb_ref, 4, surface_channel)
 
     late = (y >= SIDE // 2) | (chip == 0)
-    pl.when(jnp.logical_not(late))(all_inner)
+    def early_inner():
+        all_inner()
+
+        def cut(q, _):
+            for u in range(4):
+                first_part(q * 4 + u)
+            return 0
+
+        lax.fori_loop(0, n_chips // 4, cut, 0)
+
+    pl.when(jnp.logical_not(late))(early_inner)
     pl.semaphore_wait(barrier, n_chips + 1)
     rim_copies = []
     for side, other in ((0, right), (1, left)):
         copy = pltpu.make_async_remote_copy(
-            src_ref=rim_out,
+            src_ref=rim_out.at[side],
             dst_ref=rim_in.at[side],
             send_sem=rim_send.at[side],
             recv_sem=rim_recv.at[side],
@@ -277,102 +342,109 @@
         copy.start()
         rim_copies.append(copy)
 
-    pl.when(late)(all_inner)
+    def late_inner():
+        all_inner()
+
+        def cut_and_send(q, _):
+            for u in range(7):
+                first_part(1 + q * 7 + u)
+            for u in range(7):
+                send_copy(0, 1 + q * 7 + u).start()
+            return 0
+
+        lax.fori_loop(0, (n_chips - 1) // 7, cut_and_send, 0)
+        first_part(0)
+
+    def early_send():
+        def send_first(s, _):
+            send_copy(0, s).start()
+            return 0
+
+        lax.fori_loop(1, n_chips, send_first, 0)
+
+    pl.when(late)(late_inner)
+    pl.when(jnp.logical_not(late))(early_send)
+    own_copy(0).start()
+
 
     for copy in rim_copies:
         copy.wait()
 
     def add_rims(q, _):
-        for u in range(6):
-            t = q * 6 + u
-            before = rim_in[0, t].astype(F32)
-            after = rim_in[1, t].astype(F32)
-            image[t, 2] += jnp.where(row8 % 4 < 2, before, 0.0)
-            image[t, 0] += jnp.where(row8 >= 6, pltpu.roll(after, 4, 0), 0.0)
-            image[t, 1] += jnp.where(row8 >= 6, after, 0.0)
+        for u in range(3):
+            c = q * 3 + u
+            before = rim_in[0, c].astype(F32)
+            after = rim_in[1, c].astype(F32)
+            image[2 * c, 2] += jnp.where(low4, before, pltpu.roll(after, 2, 0))
+            image[2 * c + 1, 2] += jnp.where(low4, pltpu.roll(before, 6, 0), after)
         return 0
 
-    lax.fori_loop(0, ROWS // 6, add_rims, 0)
-
-    lane = lax.broadcasted_iota(jnp.int32, (8, 128), 1)
-
-    def send_copy(s):
-        dy, dx = offset_of(s)
-        to = ((y + dy) % SIDE) * SIDE + (x + dx) % SIDE
-        return to, pltpu.make_async_remote_copy(
-            src_ref=chunks.at[s],
-            dst_ref=got_ref.at[s],
-            send_sem=send_sem.at[s],
-            recv_sem=recv_sem.at[s],
-            device_id={"win": to * 2 + core},
-            device_id_type=MESH,
-        )
-
-    def make_chunk(s, to):
-        tails = jnp.zeros((8, 128), F32)
-        for k in range(2):
-            d = to * 2 + k
-            t = (d * ROWS) // 128
-            o = (d * ROWS) % 128
-            back = (128 - o) % 128
-            for g in range(3):
-                a = pltpu.roll(image[t, g], back, 1)
-                b = pltpu.roll(image[t + 1, g], back, 1)
-                c = pltpu.roll(image[t + 2, g], back, 1)
-                chunks[s, 4 * k + g] = jnp.where(lane < 128 - o, a, b).astype(BF)
-                tail = jnp.where(lane < 128 - o, b, c)
-                for slot in (g,) if g < 2 else (2, 3):
-                    at = 64 * k + 16 * slot
-                    moved = pltpu.roll(tail, at, 1) if at else tail
-                    tails = jnp.where((lane >= at) & (lane < at + 10), moved, tails)
-        chunks[s, 3] = tails.astype(BF)
-
-    make_chunk(0, chip)
-    got_ref[0] = chunks[0]
-
-    def exchange(q, _):
-        for u in range(3):
-            s = 1 + q * 3 + u
-            to, copy = send_copy(s)
-            make_chunk(s, to)
-            copy.start()
+    lax.fori_loop(0, CHANNELS // 3, add_rims, 0)
+
+    def send_second(q, _):
+        for u in range(7):
+            second_part(1 + q * 7 + u)
+        for u in range(7):
+            send_copy(1, 1 + q * 7 + u).start()
         return 0
 
-    lax.fori_loop(0, (n_chips - 1) // 3, exchange, 0)
-    def twin_copy(g):
-        part = pl.ds(g * SIDE, SIDE)
+    lax.fori_loop(0, (n_chips - 1) // 7, send_second, 0)
+    second_part(0)
+    own_copy(1).start()
+    for half in range(2):
+        own_copy(half).wait()
+
+    def twin_copy(half, g):
+        chips = pl.ds(g * SIDE, SIDE)
+        first = (2 * (1 - core), 4 + 1 - core)[half]
         return pltpu.make_async_remote_copy(
-            src_ref=got_ref.at[part, pl.ds(3 * (1 - core), 4)],
-            dst_ref=twin_ref.at[part],
-            send_sem=twin_send.at[g],
-            recv_sem=twin_recv.at[g],
+            src_ref=got_ref.at[chips, pl.ds(first, 2)],
+            dst_ref=twin_ref.at[chips, pl.ds(2 * half, 2)],
+            send_sem=twin_send.at[half, g],
+            recv_sem=twin_recv.at[half, g],
             device_id={"win": twin},
             device_id_type=MESH,
         )
 
-    def arrived(s, _):
-        send_copy(s)[1].wait_recv()
-        return 0
-
-    for g in range(n_chips // SIDE):
-        lax.fori_loop(max(1, g * SIDE), (g + 1) * SIDE, arrived, 0)
-        twin_copy(g).start()
-
-    def left_here(s, _):
-        send_copy(s)[1].wait_send()
-        return 0
-
-    lax.fori_loop(1, n_chips, left_here, 0)
-    for g in range(n_chips // SIDE):
-        twin_copy(g).wait()
-    finish(n_chips, y, x, core, got_ref, twin_ref, out_ref)
-
-
-def finish(n_chips, y, x, core, got_ref, twin_ref, out_ref):
+    for half in range(2):
+
+        def arrived(s, _):
+            send_copy(half, s).wait_recv()
+            return 0
+
+        for g in range(n_chips // SIDE):
+            lax.fori_loop(max(1, g * SIDE), (g + 1) * SIDE, arrived, 0)
+            twin_copy(half, g).start()
+
+    for half in range(2):
+
+        def left_here(s, _):
+            send_copy(half, s).wait_send()
+            return 0
+
+        lax.fori_loop(1, n_chips, left_here, 0)
+        for g in range(n_chips // SIDE):
+            twin_copy(half, g).wait()
+
+
+def finish(n_chips, got_any, twin_any, out_any, got_ref, twin_ref, rows_ref, in_sem, out_sem):
+    w = lax.axis_index("win")
+    chip, core = w // 2, w % 2
+    y, x = chip // SIDE, chip % SIDE
+    loads = [
+        pltpu.make_async_copy(twin_any, twin_ref, in_sem.at[0]),
+        pltpu.make_async_copy(
+            got_any.at[:, pl.ds(2 * core, 2)], got_ref.at[:, pl.ds(0, 2)], in_sem.at[1]
+        ),
+        pltpu.make_async_copy(
+            got_any.at[:, pl.ds(4 + core, 2)], got_ref.at[:, pl.ds(2, 2)], in_sem.at[2]
+        ),
+    ]
+    for load in loads:
+        load.start()
     first = core == 0
     row = lax.broadcasted_iota(jnp.int32, (8, 128), 0)
     lane = lax.broadcasted_iota(jnp.int32, (8, 128), 1)
-    top = row < 4
     spot = lane - 64 * core
     bands = ((spot >= 0) & (spot < 10)) | ((spot >= 16) & (spot < 26))
     third = (spot >= 32) & (spot < 42)
@@ -380,6 +452,13 @@
 
     def select(mask, value):
         return jnp.where(mask, value, 0.0)
+
+    def ordered(ga, gb, ra, rb):
+        middle = jnp.where(row < 4, ga, jnp.where(row < 6, gb, rb))
+        return jnp.concatenate(
+            [jnp.where(row < 2, ga, ra), jnp.where(row < 2, ra, middle), jnp.where(row < 6, rb, gb)],
+            axis=0,
+        )
 
     r = lax.broadcasted_iota(jnp.int32, (2 * ROWS, 384), 0)
     k = lax.broadcasted_iota(jnp.int32, (2 * ROWS, 384), 1)
@@ -387,66 +466,68 @@
     at = 256 + 64 * core + 16 * m + rho - 128
     hot = ((rho < 128) & (k == 128 * m + rho)) | ((rho >= 128) & ((k == at) | (k == at + 32)))
     pick = jnp.where(hot, 1.0, 0.0).astype(BF)
+    for load in loads:
+        load.wait()
+
+    def out_copy(block):
+        part = pl.ds(block * 384, 384)
+        return pltpu.make_async_copy(
+            rows_ref.at[:, :, part], out_any.at[:, :, part], out_sem.at[block]
+        )
 
     for block in range(n_chips // 16):
         pieces = []
         for i in range(16):
             p = block * 16 + i
             s = step_of((y - p // SIDE + SIDE) % SIDE, (x - p % SIDE + SIDE) % SIDE)
-            mine = [got_ref[s, 3 * core + u].astype(F32) for u in range(4)]
+            mine = [got_ref[s, u].astype(F32) for u in range(4)]
             other = [twin_ref[s, u].astype(F32) for u in range(4)]
-            mine = [jnp.where(first, mine[u], mine[(u + 1) % 4]) for u in range(4)]
-            other = [jnp.where(first, other[u], other[(u + 1) % 4]) for u in range(4)]
-            a = [jnp.where(first, mine[u], other[u]) for u in range(4)]
-            b = [jnp.where(first, other[u], mine[u]) for u in range(4)]
-            blocks = []
-            for mm in range(2):
-                ra = pltpu.roll(a[mm], 4, 0)
-                if mm == 0:
-                    rows = [
-                        jnp.where(top, a[2], ra),
-                        jnp.where(top, ra, pltpu.roll(b[2], 4, 0)),
-                        b[0],
-                    ]
-                else:
-                    rows = [
-                        jnp.where(top, pltpu.roll(a[2], 4, 0), ra),
-                        jnp.where(top, ra, b[2]),
-                        b[1],
-                    ]
-                blocks.append(jnp.concatenate(rows, axis=0))
-            ta, tb = a[3], b[3]
-            ra, rb = pltpu.roll(ta, 4, 0), pltpu.roll(tb, 4, 0)
-            rows = [
-                jnp.where(top, select(third, ta) + select(fourth, ra), select(bands, ra)),
-                jnp.where(top, select(bands, ra), select(third, rb) + select(fourth, tb)),
-                select(bands, tb),
+            a, b = [], []
+            for u in (0, 1, 2, 3):
+                v = u if u < 2 else 5 - u
+                here = jnp.where(first, mine[u], mine[v])
+                there = jnp.where(first, other[u], other[v])
+                a.append(jnp.where(first, here, there))
+                b.append(jnp.where(first, there, here))
+            ga, gb = pltpu.roll(a[2], 4, 0), pltpu.roll(b[2], 4, 0)
+            ta, tb = pltpu.roll(a[3], 4, 0), pltpu.roll(b[3], 4, 0)
+            blocks = [
+                ordered(a[2], gb, pltpu.roll(a[0], 2, 0), pltpu.roll(b[0], 6, 0)),
+                ordered(ga, b[2], pltpu.roll(a[1], 2, 0), pltpu.roll(b[1], 6, 0)),
+                ordered(
+                    select(third, a[3]) + select(fourth, ta),
+                    select(third, tb) + select(fourth, b[3]),
+                    select(bands, pltpu.roll(a[3], 2, 0)),
+                    select(bands, pltpu.roll(b[3], 6, 0)),
+                ),
             ]
-            blocks.append(jnp.concatenate(rows, axis=0))
             pieces.append(jnp.concatenate(blocks, axis=1))
         stacked = jnp.concatenate(pieces, axis=0).astype(BF)
-        out_ref[:, :, block * 384 : block * 384 + 384] = (
+        rows_ref[:, :, block * 384 : block * 384 + 384] = (
             lax.dot_general(pick, stacked, NT, preferred_element_type=F32)
             .astype(BF)
             .reshape(ROWS, 2, 384)
         )
+        out_copy(block).start()
+    for block in range(n_chips // 16):
+        out_copy(block).wait()
 
 
 def body(n_chips, tokens, w_upper, w_surface, bias):
     t = jnp.transpose(tokens, (0, 1, 3, 2, 4))
     width = t.shape[-1]
-    vmem = pl.BlockSpec(memory_space=pltpu.VMEM)
     smem = pl.BlockSpec(memory_space=pltpu.SMEM)
     hbm = pl.BlockSpec(memory_space=pl.ANY)
     dma = pltpu.SemaphoreType.DMA
-    rows = pl.pallas_call(
+    got, twin = pl.pallas_call(
         functools.partial(kernel, n_chips),
-        out_shape=jax.ShapeDtypeStruct((ROWS, 2, n_chips * 24), BF),
+        out_shape=(
+            jax.ShapeDtypeStruct((n_chips, 7, 8, 128), BF),
+            jax.ShapeDtypeStruct((n_chips, 4, 8, 128), BF),
+        ),
         in_specs=[hbm, hbm, hbm, smem],
-        out_specs=vmem,
+        out_specs=(hbm, hbm),
         scratch_shapes=[
-            pltpu.VMEM((n_chips, 7, 8, 128), BF),
-            pltpu.VMEM((n_chips, 4, 8, 128), BF),
             pltpu.VMEM(t.shape, BF),
             pltpu.VMEM(w_upper.shape, BF),
             pltpu.VMEM(w_surface.shape, BF),
@@ -461,21 +542,37 @@
             pltpu.VMEM((320, 256), F32),
             dma((t.shape[1] + 2,)),
             pltpu.VMEM((TILES, 3, 8, 128), F32),
-            pltpu.VMEM((TILES, 8, 128), BF),
-            pltpu.VMEM((2, TILES, 8, 128), BF),
+            pltpu.VMEM((2, CHANNELS, 8, 128), BF),
+            pltpu.VMEM((2, CHANNELS, 8, 128), BF),
             pltpu.VMEM((n_chips, 7, 8, 128), BF),
             dma((2,)),
             dma((2,)),
-            dma((n_chips,)),
-            dma((n_chips,)),
-            dma((n_chips // SIDE,)),
-            dma((n_chips // SIDE,)),
+            dma((2,)),
+            dma((2, n_chips)),
+            dma((2, n_chips)),
+            dma((2, n_chips // SIDE)),
+            dma((2, n_chips // SIDE)),
         ],
         compiler_params=pltpu.CompilerParams(
             collective_id=0, has_side_effects=True, vmem_limit_bytes=64 * 10**6
         ),
         name="recover",
     )(t, w_upper, w_surface, bias)
+    rows = pl.pallas_call(
+        functools.partial(finish, n_chips),
+        out_shape=jax.ShapeDtypeStruct((ROWS, 2, n_chips * 24), BF),
+        in_specs=[hbm, hbm],
+        out_specs=hbm,
+        scratch_shapes=[
+            pltpu.VMEM((n_chips, 4, 8, 128), BF),
+            pltpu.VMEM((n_chips, 4, 8, 128), BF),
+            pltpu.VMEM((ROWS, 2, n_chips * 24), BF),
+            dma((3,)),
+            dma((n_chips // 16,)),
+        ],
+        compiler_params=pltpu.CompilerParams(vmem_limit_bytes=64 * 10**6),
+        name="finish",
+    )(got, twin)
     return jnp.transpose(rows, (1, 0, 2))
 
 

time: 65.5 us -> 60.4 us (0.922)
  local copies, waits for them, and re-layouts: 2.64 us -> 0 us
  Pallas kernels: 62.7 us -> 60.3 us
    unnamed x1 -> x0, local copies, waits for them, and re-layouts: 2.64 us -> none
    pallas_call x1 -> x2, Pallas kernels: 62.7 us -> 60.3 us  [the longest x1 57.4 us: body(): pl.pallas_call(functools.partial(kernel, n_chips), out_shape=(jax.ShapeDt...]
where the time goes in v3:
time: 60.4 us; the launch traced here: 60.3 us
  Pallas kernels  60.3 us (100%)
    pallas_call x1, Pallas kernels, body(): pl.pallas_call(functools.partial(kernel, n_chips), out_shape=(jax.ShapeDt...  57.4 us
    pallas_call x1, Pallas kernels, body(): pl.pallas_call(functools.partial(finish, n_chips), out_shape=jax.ShapeDty...  2.89 us

profile of v3, /device:TPU:513, one launch (start us, length us, event | category | flops | bytes accessed | tf_op | source)
XLA Modules:
  0.0 60.3 jit_solution(15374220038036713761)
XLA Ops:
  0.0 57.4 %recover.1 = (bf16[64,7,8,128]{3,2,1,0:T(8,128)(2,1)}, bf16[64,4,8,128]{3,2,1,0:T(8,128)(2,1)}) custom-call(bf16[2,8,3,64,384]{4,3,2,1,0:T(8,128)(2,1)} %bitcast.2, bf16[384,640]{1,0:T(8,128)(2,1)} %wu_any.1, bf16[384,256]{1,0:T(8,128)(2,1)} %ws_any.1, f32[69]{0:T(128)} %bias_ref.1), custom_call_target="tpu_custom_call" | custom-call | tf_op jit(solution)/shard_map/recover/pallas_call | solution.py:522
  57.4 2.9 %finish.1 = bf16[138,2,1536]{2,1,0:T(2,128)(2,1)} custom-call(bf16[64,7,8,128]{3,2,1,0:T(8,128)(2,1)} %get-tuple-element.7.got_any, bf16[64,4,8,128]{3,2,1,0:T(8,128)(2,1)} %get-tuple-element.8.twin_any), custom_call_target="tpu_custom_call" | custom-call | tf_op jit(solution)/shard_map/finish/pallas_call | solution.py:561

commit v4 on v3

--- a/solution.py
+++ b/solution.py
@@ -211,28 +211,31 @@
                     rim_out[0, c] = jnp.where(low4, first, pltpu.roll(second, 2, 0)).astype(BF)
                     rim_out[1, c] = jnp.where(low4, pltpu.roll(first, 6, 0), second).astype(BF)
 
-    def inner(zs, a_ref, b_ref, kinds, channel):
-        three = [columns(zs, j) for j in range(3)]
-        rhs = jnp.concatenate(three, axis=1)
+    def inner(zs, w_ref, kinds, channel):
+        rhs = jnp.concatenate([columns(zs, j) for j in range(3)], axis=1)
         n = rhs.shape[0]
-        rows_a, rows_b = kinds * 8, kinds * 4
-        prod_a[: 8 * rows_a, :n] = lax.dot_general(a_ref[...], rhs, NT, preferred_element_type=F32)
-        rhs = jnp.concatenate([three[0], three[2]], axis=1)
-        prod_b[: 8 * rows_b, :n] = lax.dot_general(b_ref[...], rhs, NT, preferred_element_type=F32)
-        values = interleaved(
-            per_member(prod_a, rows_a, len(zs)) + per_member(prod_b, rows_b, len(zs))
-        )
+        rows = kinds * 8
+        prod_a[: 8 * rows, :n] = lax.dot_general(w_ref[...], rhs, NT, preferred_element_type=F32)
+        values = interleaved(per_member(prod_a, rows, len(zs)))
         for zi in range(len(zs)):
             for k in range(kinds):
                 c = channel(zi, k)
-                at = zi * rows_a + 8 * k
+                at = zi * rows + 8 * k
                 for m in range(2):
                     for h in range(2):
                         lo = h * 128
                         image[2 * c + h, m] = values[m][at : at + 8, lo : lo + 128] + bias_ref[c]
+
+    def outer(zs, w_ref, kinds, channel):
+        rhs = jnp.concatenate([columns(zs, 0), columns(zs, 2)], axis=1)
+        n = rhs.shape[0]
+        rows = kinds * 4
+        prod_b[: 8 * rows, :n] = lax.dot_general(w_ref[...], rhs, NT, preferred_element_type=F32)
+        values = interleaved(per_member(prod_b, rows, len(zs)))
+        for zi in range(len(zs)):
             for v in range(kinds // 2):
                 c0, c1 = channel(zi, 2 * v), channel(zi, 2 * v + 1)
-                for h, one, two in halves(values[2:], zi * rows_b + 8 * v):
+                for h, one, two in halves(values, zi * rows + 8 * v):
                     image[2 * c0 + h, 2] = one + bias_ref[c0]
                     image[2 * c1 + h, 2] = two + bias_ref[c1]
 
@@ -243,15 +246,17 @@
         rims((2 * p, 2 * p + 1), ur_ref, 10, lambda zi, k: 13 * (k // 2) + 2 * (2 * p + zi) + k % 2)
         return 0
 
+    def upper_channel(p):
+        return lambda zi, k: 13 * (k // 2) + 2 * (2 * p + zi) + k % 2
+
     def upper_inner(q, _):
         p = pairs - 1 - q
-        inner(
-            (2 * p, 2 * p + 1),
-            ua_ref,
-            ub_ref,
-            10,
-            lambda zi, k: 13 * (k // 2) + 2 * (2 * p + zi) + k % 2,
-        )
+        inner((2 * p, 2 * p + 1), ua_ref, 10, upper_channel(p))
+        return 0
+
+    def upper_outer(q, _):
+        p = pairs - 1 - q
+        outer((2 * p, 2 * p + 1), ub_ref, 10, upper_channel(p))
         return 0
 
     def surface_channel(zi, k):
@@ -314,7 +319,7 @@
 
     def all_inner():
         lax.fori_loop(0, pairs, upper_inner, 0)
-        inner((levels - 1,), sa_ref, sb_ref, 4, surface_channel)
+        inner((levels - 1,), sa_ref, 4, surface_channel)
 
     late = (y >= SIDE // 2) | (chip == 0)
     def early_inner():
@@ -365,6 +370,9 @@
     pl.when(late)(late_inner)
     pl.when(jnp.logical_not(late))(early_send)
     own_copy(0).start()
+
+    lax.fori_loop(0, pairs, upper_outer, 0)
+    outer((levels - 1,), sb_ref, 4, surface_channel)
 
 
     for copy in rim_copies:

time: 60.4 us -> 59.5 us (0.985)
  Pallas kernels: 60.3 us -> 59.3 us
    pallas_call x1, Pallas kernels: 57.4 us -> 56.4 us  [body(): pl.pallas_call(functools.partial(kernel, n_chips), out_shape=(jax.ShapeDt...]
where the time goes in v4:
time: 59.5 us; the launch traced here: 59.3 us
  Pallas kernels  59.3 us (100%)
    pallas_call x1, Pallas kernels, body(): pl.pallas_call(functools.partial(kernel, n_chips), out_shape=(jax.ShapeDt...  56.4 us
    pallas_call x1, Pallas kernels, body(): pl.pallas_call(functools.partial(finish, n_chips), out_shape=jax.ShapeDty...  2.89 us

profile of v4, /device:TPU:513, one launch (start us, length us, event | category | flops | bytes accessed | tf_op | source)
XLA Modules:
  0.0 59.3 jit_solution(6400840608938458494)
XLA Ops:
  0.0 56.4 %recover.1 = (bf16[64,7,8,128]{3,2,1,0:T(8,128)(2,1)}, bf16[64,4,8,128]{3,2,1,0:T(8,128)(2,1)}) custom-call(bf16[2,8,3,64,384]{4,3,2,1,0:T(8,128)(2,1)} %bitcast.2, bf16[384,640]{1,0:T(8,128)(2,1)} %wu_any.1, bf16[384,256]{1,0:T(8,128)(2,1)} %ws_any.1, f32[69]{0:T(128)} %bias_ref.1), custom_call_target="tpu_custom_call" | custom-call | tf_op jit(solution)/shard_map/recover/pallas_call | solution.py:530
  56.4 2.9 %finish.1 = bf16[138,2,1536]{2,1,0:T(2,128)(2,1)} custom-call(bf16[64,7,8,128]{3,2,1,0:T(8,128)(2,1)} %get-tuple-element.7.got_any, bf16[64,4,8,128]{3,2,1,0:T(8,128)(2,1)} %get-tuple-element.8.twin_any), custom_call_target="tpu_custom_call" | custom-call | tf_op jit(solution)/shard_map/finish/pallas_call | solution.py:569
